TPU v7x, 32 devices: a whole 2x2x4 slice. The times are simulated.
32 devices in a mesh: grp: 2 (over y), gx: 16 (over z, x, core), gy: 1.
Axes of the slice: x: 2, y: 2, z: 4, core: 2. Of those that a mesh axis runs over, the one named last changes fastest.
Arguments:
- residue_feats: bfloat16 [512, 256], P(('grp', 'gx')), parts along dimension 0, may hold values from -6 to 6
- pair_feats: bfloat16 [64, 512, 256], P(None, ('grp', 'gx'), 'gy'), parts along dimension 1, may hold values from -30 to 30
- w_row: bfloat16 [256, 64], replicated, may hold values from -0.375 to 0.375
- w_col: bfloat16 [256, 64], replicated, may hold values from -0.375 to 0.375
- first_taps: bfloat16 [9, 64, 64], replicated, may hold values from -0.25 to 0.25
- second_taps: bfloat16 [9, 64, 64], replicated, may hold values from -0.25 to 0.25
- norm_scale: float32 [2, 64], replicated, may hold values from 0.25 to 1.75
- norm_shift: float32 [2, 64], replicated, may hold values from -2 to 2
Outputs:
- symmetric: bfloat16 [64, 512, 256], P(None, ('grp', 'gx'), 'gy'), parts along dimension 1
There are 2 independent parts, one for each index of `grp`. A program takes and returns all parts, laid end to end along the dimension named above; an argument that names none is the same for every part. Nothing has to cross between parts.
All inputs are finite; a program needn't handle non-finite values.
Results may differ from a plain program's by a relative error of at most 0.012.
Values may be sent and summed in bfloat16 or wider, within the bound.
A program may use at most 64 MiB of HBM per device.

v0:
```python
import jax
import jax.numpy as jnp
from jax import lax
from jax.sharding import PartitionSpec as P

DILATION_STEP = 8
epsilon = 1e-05


def with_halo(cells, sides, width):
    for axis, dim in sides:
        count = lax.axis_size(axis)
        ends = count - 1
        head = lax.slice_in_dim(cells, 0, width, axis=dim)
        tail = lax.slice_in_dim(cells, cells.shape[dim] - width, cells.shape[dim], axis=dim)
        cells = jnp.concatenate(
            [
                lax.ppermute(tail, axis, [(i, (i + 1) % count) for i in range(ends)]),
                cells,
                lax.ppermute(head, axis, [((i + 1) % count, i) for i in range(ends)]),
            ],
            axis=dim,
        )
    return cells


def dilated(receptive_region, weights):
    row_count = receptive_region.shape[1]
    col_count = receptive_region.shape[2]
    border_padded_input = with_halo(receptive_region, (("gx", 1), ("gy", 2)), DILATION_STEP)
    tap_sum_total = jnp.zeros((weights.shape[1], row_count, col_count), jnp.float32)
    for filter_tap_index in range(9):
        row_displacement = filter_tap_index // 3 * DILATION_STEP
        column_displacement = filter_tap_index % 3 * DILATION_STEP
        window = border_padded_input[
            :,
            row_displacement : row_displacement + row_count,
            column_displacement : column_displacement + col_count,
        ]
        tap_sum_total = tap_sum_total + jnp.einsum(
            "oc,crw->orw", weights[filter_tap_index], window, preferred_element_type=jnp.float32
        )
    return tap_sum_total


def normalized(tap_sum_total, gain, shift):
    cell_count = (
        tap_sum_total.shape[1] * tap_sum_total.shape[2] * lax.axis_size("gx") * lax.axis_size("gy")
    )
    first_sum, second_sum = lax.psum(
        (jnp.sum(tap_sum_total, axis=(1, 2)), jnp.sum(tap_sum_total * tap_sum_total, axis=(1, 2))),
        ("gx", "gy"),
    )
    average = first_sum / cell_count
    spread = second_sum / cell_count - average * average
    centred = tap_sum_total - average[:, None, None]
    factor = gain * lax.rsqrt(spread + epsilon)
    return centred * factor[:, None, None] + shift[:, None, None]


def body(residue_feats, pair_feats, w_row, w_col, first_taps, second_taps, norm_scale, norm_shift):
    col_count = pair_feats.shape[2]
    col_start = lax.axis_index("gy") * col_count
    row_part = jnp.dot(residue_feats, w_row, preferred_element_type=jnp.float32).astype(
        jnp.bfloat16
    )
    everyone = lax.all_gather(residue_feats, "gx", axis=0, tiled=True)
    col_feats = lax.dynamic_slice_in_dim(everyone, col_start, col_count, 0)
    col_part = jnp.dot(col_feats, w_col, preferred_element_type=jnp.float32).astype(jnp.bfloat16)
    block_in = (
        pair_feats.astype(jnp.float32)
        + row_part.T.astype(jnp.float32)[:, :, None]
        + col_part.T.astype(jnp.float32)[:, None, :]
    ).astype(jnp.bfloat16)
    first_conv = dilated(block_in, first_taps)
    activated = jax.nn.elu(normalized(first_conv, norm_scale[0], norm_shift[0])).astype(
        jnp.bfloat16
    )
    second_conv = dilated(activated, second_taps)
    block_out = jax.nn.elu(
        block_in.astype(jnp.float32) + normalized(second_conv, norm_scale[1], norm_shift[1])
    ).astype(jnp.bfloat16)
    whole_rows = lax.all_gather(block_out, "gy", axis=2, tiled=True)
    columns = lax.all_to_all(whole_rows, "gx", split_axis=2, concat_axis=1, tiled=True)
    flipped = lax.dynamic_slice_in_dim(columns, col_start, col_count, 1)
    mirrored = jnp.transpose(flipped, (0, 2, 1))
    return (0.5 * (block_out.astype(jnp.float32) + mirrored.astype(jnp.float32))).astype(
        jnp.bfloat16
    )


def solution(mesh):
    placed = (P(("grp", "gx"), None), P(None, ("grp", "gx"), "gy"), P(), P(), P(), P(), P(), P())
    return jax.shard_map(
        body, mesh=mesh, in_specs=placed, out_specs=P(None, ("grp", "gx"), "gy"), check_vma=False
    )
```

profile of v0, /device:TPU:0, one launch (start us, length us, event | category | flops | bytes accessed | tf_op | source)
XLA Modules:
  0.0 140.1 jit_solution(18333366935052121485)
XLA Ops:
  0.0 23.8 %all_gather.4 = bf16[256,256]{1,0:T(8,128)(2,1)S(1)} all-gather(bf16[16,256]{1,0:T(8,128)(2,1)} %param.8), channel_id=1, replica_groups=mesh['grp'=2,'gx'=16,'gy'=1] {'gx'}, dimensions={0}, use_global_device_ids=true | all-gather | bytes 139264 | tf_op jit(solution)/shard_map/all_gather | solution.py:67
  23.8 0.9 fusion.13
  24.9 1.3 add_convert_fusion
  26.2 2.3 %collective-permute-start = (bf16[64,8,256]{2,0,1:T(8,128)(2,1)S(1)}, bf16[64,8,256]{2,0,1:T(8,128)(2,1)S(1)}, u32[]{:S(2)}, u32[]{:S(2)}) collective-permute-start(bf16[64,8,256]{2,0,1:T(8,128)(2,1)S(1)} %get-tuple-element.23), channel_id=1, source_target_pairs={{0,1},{1,2},{2,3},{3,4},{4,5},{5,6},{6,7},{7,8},{8,9},{9,10},{10,1... | collective-permute-start | bytes 786440 | tf_op jit(solution)/shard_map/ppermute | solution.py:18
  28.5 1.3 collective-permute-start.1
  30.1 1.8 %collective-permute-done.1 = bf16[64,8,256]{2,0,1:T(8,128)(2,1)S(1)} collective-permute-done((bf16[64,8,256]{2,0,1:T(8,128)(2,1)S(1)}, bf16[64,8,256]{2,0,1:T(8,128)(2,1)S(1)}, u32[]{:S(2)}, u32[]{:S(2)}) %collective-permute-start.1) | collective-permute-done | bytes 262176 | tf_op jit(solution)/shard_map/ppermute | solution.py:20
  32.3 0.7 collective-permute-start.2
  33.0 0.7 collective-permute-start.3
  34.3 1.3 maximum_maximum_fusion
  38.0 33.9 %all-reduce.1 = (f32[64]{0:T(128)S(1)}, f32[64]{0:T(128)S(1)}) all-reduce(f32[64]{0:T(128)S(1)} %get-tuple-element.8, f32[64]{0:T(128)S(1)} %get-tuple-element.7), channel_id=1, replica_groups=mesh['grp'=2,'gx'=16,'gy'=1] {'gx','gy'}, use_global_device_ids=true, to_apply=%region_3.0 | all-reduce | flops 128 | bytes 1024 | tf_op jit(solution)/shard_map/psum | solution.py:50
  72.6 1.3 collective-permute-start.4
  73.9 1.3 collective-permute-start.5
  75.5 1.8 %collective-permute-done.5 = bf16[64,8,256]{2,0,1:T(8,128)(2,1)S(1)} collective-permute-done((bf16[64,8,256]{2,0,1:T(8,128)(2,1)S(1)}, bf16[64,8,256]{2,0,1:T(8,128)(2,1)S(1)}, u32[]{:S(2)}, u32[]{:S(2)}) %collective-permute-start.5) | collective-permute-done | bytes 262176 | tf_op jit(solution)/shard_map/ppermute | solution.py:20
  77.8 0.7 collective-permute-start.6
  78.5 0.7 collective-permute-start.7
  79.7 1.3 maximum_maximum_fusion.1
  83.4 31.5 %all-reduce = (f32[64]{0:T(128)S(1)}, f32[64]{0:T(128)S(1)}) all-reduce(f32[64]{0:T(128)S(1)} %get-tuple-element.6, f32[64]{0:T(128)S(1)} %get-tuple-element.5), channel_id=1, replica_groups=mesh['grp'=2,'gx'=16,'gy'=1] {'gx','gy'}, use_global_device_ids=true, to_apply=%region_7.8 | all-reduce | flops 128 | bytes 1024 | tf_op jit(solution)/shard_map/psum | solution.py:50
  115.0 0.7 fusion.17
  115.7 1.0 copy.18
  116.7 0.7 reshape.32
  117.4 16.9 %all_to_all.4 = bf16[16,2,8192]{2,1,0:T(2,128)(2,1)S(1)} all-to-all(bf16[16,2,8192]{2,1,0:T(2,128)(2,1)S(1)} %reshape.32), channel_id=1, replica_groups=mesh['grp'=2,'gx'=16,'gy'=1] {'gx'}, dimensions={0} | all-to-all | bytes 1048576 | tf_op jit(solution)/shard_map/all_to_all | solution.py:84
  135.7 2.0 %copy.21 = f32[64,256,16]{1,0,2:T(8,128)} copy(f32[64,256,16]{0,2,1:T(8,128)S(1)} %bitcast.109) | data formatting | bytes 2097152 | tf_op jit(solution)/shard_map/convert_element_type | solution.py:87
  137.6 1.4 fusion.19
  139.0 1.1 copy.22
  (51 shorter events, 9.4 us)
Async XLA Ops:
  0.0 24.7 %copy-start = (bf16[256,64]{0,1:T(8,128)(2,1)S(1)}, bf16[256,64]{0,1:T(8,128)(2,1)}, u32[]{:S(2)}) copy-start(bf16[256,64]{0,1:T(8,128)(2,1)} %param.11) | copy-start | bytes 98308
  0.0 29.8 %copy-start.5 = (f32[2,64]{1,0:T(2,128)S(1)}, f32[2,64]{1,0:T(2,128)}, u32[]{:S(2)}) copy-start(f32[2,64]{1,0:T(2,128)} %param.15) | copy-start | bytes 1540
  0.0 29.8 %copy-start.2 = (bf16[9,64,64]{2,1,0:T(8,128)(2,1)S(1)}, bf16[9,64,64]{2,1,0:T(8,128)(2,1)}, u32[]{:S(2)}) copy-start(bf16[9,64,64]{2,1,0:T(8,128)(2,1)} %param.12) | copy-start | bytes 221188
  26.2 3.9 %collective-permute-start = (bf16[64,8,256]{2,0,1:T(8,128)(2,1)S(1)}, bf16[64,8,256]{2,0,1:T(8,128)(2,1)S(1)}, u32[]{:S(2)}, u32[]{:S(2)}) collective-permute-start(bf16[64,8,256]{2,0,1:T(8,128)(2,1)S(1)} %get-tuple-element.23), channel_id=1, source_target_pairs={{0,1},{1,2},{2,3},{3,4},{4,5},{5,6},{6,7},{7,8},{8,9},{9,10},{10,1... | collective-permute-start | bytes 786440 | tf_op jit(solution)/shard_map/ppermute | solution.py:18
  28.5 3.4 %collective-permute-start.1 = (bf16[64,8,256]{2,0,1:T(8,128)(2,1)S(1)}, bf16[64,8,256]{2,0,1:T(8,128)(2,1)S(1)}, u32[]{:S(2)}, u32[]{:S(2)}) collective-permute-start(bf16[64,8,256]{2,0,1:T(8,128)(2,1)S(1)} %get-tuple-element.24), channel_id=1, source_target_pairs={{1,0},{2,1},{3,2},{4,3},{5,4},{6,5},{7,6},{8,7},{9,8},{10,9},{11,1... | collective-permute-start | bytes 786440 | tf_op jit(solution)/shard_map/ppermute | solution.py:20
  32.3 1.9 %collective-permute-start.2 = (bf16[64,32,8]{2,0,1:T(8,128)(2,1)S(1)}, bf16[64,32,8]{2,0,1:T(8,128)(2,1)S(1)}, u32[]{:S(2)}, u32[]{:S(2)}) collective-permute-start(bf16[64,32,8]{2,0,1:T(8,128)(2,1)S(1)} %get-tuple-element.19), channel_id=1, source_target_pairs={} | collective-permute-start | bytes 98312 | tf_op jit(solution)/shard_map/ppermute | solution.py:18
  33.0 1.3 collective-permute-start.3
  37.3 34.6 %copy-start.4 = (f32[2,64]{1,0:T(2,128)S(1)}, f32[2,64]{1,0:T(2,128)}, u32[]{:S(2)}) copy-start(f32[2,64]{1,0:T(2,128)} %param.14) | copy-start | bytes 1540
  38.0 37.2 %copy-start.3 = (bf16[9,64,64]{2,1,0:T(8,128)(2,1)S(1)}, bf16[9,64,64]{2,1,0:T(8,128)(2,1)}, u32[]{:S(2)}) copy-start(bf16[9,64,64]{2,1,0:T(8,128)(2,1)} %param.13) | copy-start | bytes 221188
  72.6 2.9 %collective-permute-start.4 = (bf16[64,8,256]{2,0,1:T(8,128)(2,1)S(1)}, bf16[64,8,256]{2,0,1:T(8,128)(2,1)S(1)}, u32[]{:S(2)}, u32[]{:S(2)}) collective-permute-start(bf16[64,8,256]{2,0,1:T(8,128)(2,1)S(1)} %get-tuple-element.21), channel_id=1, source_target_pairs={{0,1},{1,2},{2,3},{3,4},{4,5},{5,6},{6,7},{7,8},{8,9},{9,10},{10,1... | collective-permute-start | bytes 786440 | tf_op jit(solution)/shard_map/ppermute | solution.py:18
  73.9 3.4 %collective-permute-start.5 = (bf16[64,8,256]{2,0,1:T(8,128)(2,1)S(1)}, bf16[64,8,256]{2,0,1:T(8,128)(2,1)S(1)}, u32[]{:S(2)}, u32[]{:S(2)}) collective-permute-start(bf16[64,8,256]{2,0,1:T(8,128)(2,1)S(1)} %get-tuple-element.22), channel_id=1, source_target_pairs={{1,0},{2,1},{3,2},{4,3},{5,4},{6,5},{7,6},{8,7},{9,8},{10,9},{11,1... | collective-permute-start | bytes 786440 | tf_op jit(solution)/shard_map/ppermute | solution.py:20
  77.8 1.9 %collective-permute-start.6 = (bf16[64,32,8]{2,0,1:T(8,128)(2,1)S(1)}, bf16[64,32,8]{2,0,1:T(8,128)(2,1)S(1)}, u32[]{:S(2)}, u32[]{:S(2)}) collective-permute-start(bf16[64,32,8]{2,0,1:T(8,128)(2,1)S(1)} %get-tuple-element.15), channel_id=1, source_target_pairs={} | collective-permute-start | bytes 98312 | tf_op jit(solution)/shard_map/ppermute | solution.py:18
  78.5 1.3 collective-permute-start.7
  82.7 32.2 %copy-start.1 = (bf16[64,16,256]{2,1,0:T(8,128)(2,1)S(1)}, bf16[64,16,256]{2,1,0:T(8,128)(2,1)}, u32[]{:S(2)}) copy-start(bf16[64,16,256]{2,1,0:T(8,128)(2,1)} %param.9) | copy-start | bytes 1572868
where the time goes:
time: 141 us; the launch traced here: 140 us
  blocking collectives  106 us (75%)
  starting transfers between devices  8.9 us (6%)
  matrix products  7.38 us (5%)
  other arithmetic  7.08 us (5%)
  local copies, waits for them, and re-layouts  6.52 us (5%)
  waiting for transfers between devices  3.66 us (3%)
    psum x2, blocking collectives, normalized(): lax.psum((jnp.sum(tap_sum_total, axis=(1, 2)), jnp.sum(tap_sum_total * ta...  65.5 us
    all_gather x1, blocking collectives, body(): everyone = lax.all_gather(residue_feats, 'gx', axis=0, tiled=True)  23.8 us
    all_to_all x1, blocking collectives, body(): lax.all_to_all(whole_rows, 'gx', split_axis=2, concat_axis=1, tiled=True)  16.9 us
    dot_general x18, matrix products, dilated(): jnp.einsum('oc,crw->orw', weights[filter_tap_index], window, preferred_el...  6.34 us
    ppermute x4, starting transfers between devices, with_halo(): lax.ppermute(tail, axis, [(i, (i + 1) % count) for i in range(ends)])  4.94 us
    ppermute x4, starting transfers between devices, with_halo(): lax.ppermute(head, axis, [((i + 1) % count, i) for i in range(ends)])  3.96 us
    ppermute x4, waiting for transfers between devices, with_halo(): lax.ppermute(head, axis, [((i + 1) % count, i) for i in range(ends)])  3.65 us
    concatenate x4, other arithmetic, with_halo(): jnp.concatenate([lax.ppermute(tail, axis, [(i, (i + 1) % count) for i in...  2.87 us
  transfers between devices with their start and end apart: 8, of which 2 were waited for; matrix products, arithmetic and copies ran while one was open for 1% of the time, Pallas kernels for 0%

commit v1 on v0

--- a/solution.py
+++ b/solution.py
@@ -48,8 +48,14 @@
         tap_sum_total.shape[1] * tap_sum_total.shape[2] * lax.axis_size("gx") * lax.axis_size("gy")
     )
     first_sum, second_sum = lax.psum(
-        (jnp.sum(tap_sum_total, axis=(1, 2)), jnp.sum(tap_sum_total * tap_sum_total, axis=(1, 2))),
-        ("gx", "gy"),
+        lax.psum(
+            (
+                jnp.sum(tap_sum_total, axis=(1, 2)),
+                jnp.sum(tap_sum_total * tap_sum_total, axis=(1, 2)),
+            ),
+            "gy",
+        ),
+        "gx",
     )
     average = first_sum / cell_count
     spread = second_sum / cell_count - average * average

time: 141 us -> 141 us (level)
  no operation moved by 1% of the time
where the time goes in v1:
time: 141 us; the launch traced here: 140 us
  blocking collectives  106 us (75%)
  starting transfers between devices  8.9 us (6%)
  matrix products  7.38 us (5%)
  other arithmetic  7.08 us (5%)
  local copies, waits for them, and re-layouts  6.52 us (5%)
  waiting for transfers between devices  3.66 us (3%)
    psum x2, blocking collectives, normalized(): lax.psum(lax.psum((jnp.sum(tap_sum_total, axis=(1, 2)), jnp.sum(tap_sum_t...  65.5 us
    all_gather x1, blocking collectives, body(): everyone = lax.all_gather(residue_feats, 'gx', axis=0, tiled=True)  23.8 us
    all_to_all x1, blocking collectives, body(): lax.all_to_all(whole_rows, 'gx', split_axis=2, concat_axis=1, tiled=True)  16.9 us
    dot_general x18, matrix products, dilated(): jnp.einsum('oc,crw->orw', weights[filter_tap_index], window, preferred_el...  6.34 us
    ppermute x4, starting transfers between devices, with_halo(): lax.ppermute(tail, axis, [(i, (i + 1) % count) for i in range(ends)])  4.94 us
    ppermute x4, starting transfers between devices, with_halo(): lax.ppermute(head, axis, [((i + 1) % count, i) for i in range(ends)])  3.96 us
    ppermute x4, waiting for transfers between devices, with_halo(): lax.ppermute(head, axis, [((i + 1) % count, i) for i in range(ends)])  3.65 us
    concatenate x4, other arithmetic, with_halo(): jnp.concatenate([lax.ppermute(tail, axis, [(i, (i + 1) % count) for i in...  2.87 us
  transfers between devices with their start and end apart: 8, of which 2 were waited for; matrix products, arithmetic and copies ran while one was open for 1% of the time, Pallas kernels for 0%

profile of v1, /device:TPU:0, one launch (start us, length us, event | category | flops | bytes accessed | tf_op | source)
XLA Modules:
  0.0 140.1 jit_solution(18333366935052121485)
XLA Ops:
  0.0 23.8 %all_gather.4 = bf16[256,256]{1,0:T(8,128)(2,1)S(1)} all-gather(bf16[16,256]{1,0:T(8,128)(2,1)} %param.8), channel_id=1, replica_groups=mesh['grp'=2,'gx'=16,'gy'=1] {'gx'}, dimensions={0}, use_global_device_ids=true | all-gather | bytes 139264 | tf_op jit(solution)/shard_map/all_gather | solution.py:73
  23.8 0.9 fusion.13
  24.9 1.3 add_convert_fusion
  26.2 2.3 %collective-permute-start = (bf16[64,8,256]{2,0,1:T(8,128)(2,1)S(1)}, bf16[64,8,256]{2,0,1:T(8,128)(2,1)S(1)}, u32[]{:S(2)}, u32[]{:S(2)}) collective-permute-start(bf16[64,8,256]{2,0,1:T(8,128)(2,1)S(1)} %get-tuple-element.23), channel_id=1, source_target_pairs={{0,1},{1,2},{2,3},{3,4},{4,5},{5,6},{6,7},{7,8},{8,9},{9,10},{10,1... | collective-permute-start | bytes 786440 | tf_op jit(solution)/shard_map/ppermute | solution.py:18
  28.5 1.3 collective-permute-start.1
  30.1 1.8 %collective-permute-done.1 = bf16[64,8,256]{2,0,1:T(8,128)(2,1)S(1)} collective-permute-done((bf16[64,8,256]{2,0,1:T(8,128)(2,1)S(1)}, bf16[64,8,256]{2,0,1:T(8,128)(2,1)S(1)}, u32[]{:S(2)}, u32[]{:S(2)}) %collective-permute-start.1) | collective-permute-done | bytes 262176 | tf_op jit(solution)/shard_map/ppermute | solution.py:20
  32.3 0.7 collective-permute-start.2
  33.0 0.7 collective-permute-start.3
  34.3 1.3 maximum_maximum_fusion
  38.0 33.9 %all-reduce.1 = (f32[64]{0:T(128)S(1)}, f32[64]{0:T(128)S(1)}) all-reduce(f32[64]{0:T(128)S(1)} %get-tuple-element.8, f32[64]{0:T(128)S(1)} %get-tuple-element.7), channel_id=1, replica_groups=mesh['grp'=2,'gx'=16,'gy'=1] {'gx'}, use_global_device_ids=true, to_apply=%region_3.0 | all-reduce | flops 128 | bytes 1024 | tf_op jit(solution)/shard_map/psum | solution.py:50
  72.6 1.3 collective-permute-start.4
  73.9 1.3 collective-permute-start.5
  75.5 1.8 %collective-permute-done.5 = bf16[64,8,256]{2,0,1:T(8,128)(2,1)S(1)} collective-permute-done((bf16[64,8,256]{2,0,1:T(8,128)(2,1)S(1)}, bf16[64,8,256]{2,0,1:T(8,128)(2,1)S(1)}, u32[]{:S(2)}, u32[]{:S(2)}) %collective-permute-start.5) | collective-permute-done | bytes 262176 | tf_op jit(solution)/shard_map/ppermute | solution.py:20
  77.8 0.7 collective-permute-start.6
  78.5 0.7 collective-permute-start.7
  79.7 1.3 maximum_maximum_fusion.1
  83.4 31.5 %all-reduce = (f32[64]{0:T(128)S(1)}, f32[64]{0:T(128)S(1)}) all-reduce(f32[64]{0:T(128)S(1)} %get-tuple-element.6, f32[64]{0:T(128)S(1)} %get-tuple-element.5), channel_id=1, replica_groups=mesh['grp'=2,'gx'=16,'gy'=1] {'gx'}, use_global_device_ids=true, to_apply=%region_7.8 | all-reduce | flops 128 | bytes 1024 | tf_op jit(solution)/shard_map/psum | solution.py:50
  115.0 0.7 fusion.17
  115.7 1.0 copy.18
  116.7 0.7 reshape.32
  117.4 16.9 %all_to_all.4 = bf16[16,2,8192]{2,1,0:T(2,128)(2,1)S(1)} all-to-all(bf16[16,2,8192]{2,1,0:T(2,128)(2,1)S(1)} %reshape.32), channel_id=1, replica_groups=mesh['grp'=2,'gx'=16,'gy'=1] {'gx'}, dimensions={0} | all-to-all | bytes 1048576 | tf_op jit(solution)/shard_map/all_to_all | solution.py:90
  135.7 2.0 %copy.21 = f32[64,256,16]{1,0,2:T(8,128)} copy(f32[64,256,16]{0,2,1:T(8,128)S(1)} %bitcast.109) | data formatting | bytes 2097152 | tf_op jit(solution)/shard_map/convert_element_type | solution.py:93
  137.6 1.4 fusion.19
  139.0 1.1 copy.22
  (51 shorter events, 9.4 us)
Async XLA Ops:
  0.0 24.7 %copy-start = (bf16[256,64]{0,1:T(8,128)(2,1)S(1)}, bf16[256,64]{0,1:T(8,128)(2,1)}, u32[]{:S(2)}) copy-start(bf16[256,64]{0,1:T(8,128)(2,1)} %param.11) | copy-start | bytes 98308
  0.0 29.8 %copy-start.5 = (f32[2,64]{1,0:T(2,128)S(1)}, f32[2,64]{1,0:T(2,128)}, u32[]{:S(2)}) copy-start(f32[2,64]{1,0:T(2,128)} %param.15) | copy-start | bytes 1540
  0.0 29.8 %copy-start.2 = (bf16[9,64,64]{2,1,0:T(8,128)(2,1)S(1)}, bf16[9,64,64]{2,1,0:T(8,128)(2,1)}, u32[]{:S(2)}) copy-start(bf16[9,64,64]{2,1,0:T(8,128)(2,1)} %param.12) | copy-start | bytes 221188
  26.2 3.9 %collective-permute-start = (bf16[64,8,256]{2,0,1:T(8,128)(2,1)S(1)}, bf16[64,8,256]{2,0,1:T(8,128)(2,1)S(1)}, u32[]{:S(2)}, u32[]{:S(2)}) collective-permute-start(bf16[64,8,256]{2,0,1:T(8,128)(2,1)S(1)} %get-tuple-element.23), channel_id=1, source_target_pairs={{0,1},{1,2},{2,3},{3,4},{4,5},{5,6},{6,7},{7,8},{8,9},{9,10},{10,1... | collective-permute-start | bytes 786440 | tf_op jit(solution)/shard_map/ppermute | solution.py:18
  28.5 3.4 %collective-permute-start.1 = (bf16[64,8,256]{2,0,1:T(8,128)(2,1)S(1)}, bf16[64,8,256]{2,0,1:T(8,128)(2,1)S(1)}, u32[]{:S(2)}, u32[]{:S(2)}) collective-permute-start(bf16[64,8,256]{2,0,1:T(8,128)(2,1)S(1)} %get-tuple-element.24), channel_id=1, source_target_pairs={{1,0},{2,1},{3,2},{4,3},{5,4},{6,5},{7,6},{8,7},{9,8},{10,9},{11,1... | collective-permute-start | bytes 786440 | tf_op jit(solution)/shard_map/ppermute | solution.py:20
  32.3 1.9 %collective-permute-start.2 = (bf16[64,32,8]{2,0,1:T(8,128)(2,1)S(1)}, bf16[64,32,8]{2,0,1:T(8,128)(2,1)S(1)}, u32[]{:S(2)}, u32[]{:S(2)}) collective-permute-start(bf16[64,32,8]{2,0,1:T(8,128)(2,1)S(1)} %get-tuple-element.19), channel_id=1, source_target_pairs={} | collective-permute-start | bytes 98312 | tf_op jit(solution)/shard_map/ppermute | solution.py:18
  33.0 1.3 collective-permute-start.3
  37.3 34.6 %copy-start.4 = (f32[2,64]{1,0:T(2,128)S(1)}, f32[2,64]{1,0:T(2,128)}, u32[]{:S(2)}) copy-start(f32[2,64]{1,0:T(2,128)} %param.14) | copy-start | bytes 1540
  38.0 37.2 %copy-start.3 = (bf16[9,64,64]{2,1,0:T(8,128)(2,1)S(1)}, bf16[9,64,64]{2,1,0:T(8,128)(2,1)}, u32[]{:S(2)}) copy-start(bf16[9,64,64]{2,1,0:T(8,128)(2,1)} %param.13) | copy-start | bytes 221188
  72.6 2.9 %collective-permute-start.4 = (bf16[64,8,256]{2,0,1:T(8,128)(2,1)S(1)}, bf16[64,8,256]{2,0,1:T(8,128)(2,1)S(1)}, u32[]{:S(2)}, u32[]{:S(2)}) collective-permute-start(bf16[64,8,256]{2,0,1:T(8,128)(2,1)S(1)} %get-tuple-element.21), channel_id=1, source_target_pairs={{0,1},{1,2},{2,3},{3,4},{4,5},{5,6},{6,7},{7,8},{8,9},{9,10},{10,1... | collective-permute-start | bytes 786440 | tf_op jit(solution)/shard_map/ppermute | solution.py:18
  73.9 3.4 %collective-permute-start.5 = (bf16[64,8,256]{2,0,1:T(8,128)(2,1)S(1)}, bf16[64,8,256]{2,0,1:T(8,128)(2,1)S(1)}, u32[]{:S(2)}, u32[]{:S(2)}) collective-permute-start(bf16[64,8,256]{2,0,1:T(8,128)(2,1)S(1)} %get-tuple-element.22), channel_id=1, source_target_pairs={{1,0},{2,1},{3,2},{4,3},{5,4},{6,5},{7,6},{8,7},{9,8},{10,9},{11,1... | collective-permute-start | bytes 786440 | tf_op jit(solution)/shard_map/ppermute | solution.py:20
  77.8 1.9 %collective-permute-start.6 = (bf16[64,32,8]{2,0,1:T(8,128)(2,1)S(1)}, bf16[64,32,8]{2,0,1:T(8,128)(2,1)S(1)}, u32[]{:S(2)}, u32[]{:S(2)}) collective-permute-start(bf16[64,32,8]{2,0,1:T(8,128)(2,1)S(1)} %get-tuple-element.15), channel_id=1, source_target_pairs={} | collective-permute-start | bytes 98312 | tf_op jit(solution)/shard_map/ppermute | solution.py:18
  78.5 1.3 collective-permute-start.7
  82.7 32.2 %copy-start.1 = (bf16[64,16,256]{2,1,0:T(8,128)(2,1)S(1)}, bf16[64,16,256]{2,1,0:T(8,128)(2,1)}, u32[]{:S(2)}) copy-start(bf16[64,16,256]{2,1,0:T(8,128)(2,1)} %param.9) | copy-start | bytes 1572868
